TPU v7x, 32 devices: a whole 2x2x4 slice. The times are simulated.
32 devices in a mesh: tm: 8 (over z, y), coef: 4 (over x, core).
Axes of the slice: x: 2, y: 2, z: 4, core: 2. Of those that a mesh axis runs over, the one named last changes fastest.
Arguments:
- design: bfloat16 [2048, 50176], P('tm', 'coef'), may hold values from -0.0390625 to 0.0390625
- observed: float32 [2048, 128], P('tm'), may hold values from -6 to 6
- slab_counts: int32 [8], P('tm'), may hold values from 128 to 256, as said below
- gap_mask: int32 [2048], P('tm'), may hold values 0 or 1
- filter_taps: float32 [128], replicated, may hold values from -0.5 to 1.2, as said below
- kaula_diag: float32 [50176], P('coef'), may hold values from 0.1 to 1
- precond: float32 [50176], P('coef'), may hold values from 0.3 to 3
Outputs:
- solution: float32 [50176, 128], P(('coef', 'tm'))
- residual: float32 [50176, 128], P(('coef', 'tm'))
Inputs may be any that keep to these rules, and one draw needn't show every extreme that they name: `slab_counts`: every slab holds at most 256 valid epochs, and some slab holds exactly 256. filter_taps[0] lies between 1 and 1.2.
All inputs are finite; a program needn't handle non-finite values. No bound on the sum of `gap_mask` on one device may be relied on, other than what follows from the above.
Results may differ from a plain program's by a relative error of at most 0.0065.
The roundings to bfloat16 on the way count: a program that leaves them out, or rounds other values in their place, can miss the bound.
Values may be sent and summed in bfloat16 or wider, within the bound.
No kernel may reach another device: no remote copies, remote signals or barrier semaphores. Data moves between devices by JAX's collectives and lax.ppermute only.
A program may use at most 64 MiB of HBM per device.

v0:
```python
import jax
import jax.numpy as jnp
from jax import lax
from jax.sharding import PartitionSpec as P

ITERS = 2


def shifted(value, axis, steps):
    count = lax.axis_size(axis)
    first, last = (max(0, -steps), min(count, count - steps))
    return lax.ppermute(value, axis, [(source, source + steps) for source in range(first, last)])


def toeplitz(pattern, band_len):
    tiled = jnp.tile(pattern, band_len)[: band_len * (2 * band_len - 1)]
    return tiled.reshape(band_len, 2 * band_len - 1)[:, :band_len]


def block_pair(filter_taps):
    band_len = filter_taps.shape[0]
    spacer = jnp.zeros((band_len,), jnp.float32)
    reversed_taps = filter_taps[:0:-1]
    lower = jnp.concatenate([filter_taps[:1], spacer, reversed_taps])
    upper = jnp.concatenate([jnp.zeros((1,), jnp.float32), reversed_taps, spacer])
    return (toeplitz(lower, band_len), toeplitz(upper, band_len))


def forward(values, lower_block, upper_block):
    band_len = lower_block.shape[0]
    blocks = values.reshape(-1, band_len, values.shape[1])
    tail_block = shifted(blocks[-1], "tm", 1)
    previous = jnp.concatenate([tail_block[None], blocks[:-1]], 0)
    result = jnp.einsum("ij,bjr->bir", lower_block, blocks, precision=lax.Precision.HIGHEST)
    result = result + jnp.einsum(
        "ij,bjr->bir", upper_block, previous, precision=lax.Precision.HIGHEST
    )
    return result.reshape(values.shape)


def backward(values, lower_block, upper_block):
    band_len = lower_block.shape[0]
    blocks = values.reshape(-1, band_len, values.shape[1])
    head_block = shifted(blocks[0], "tm", -1)
    following = jnp.concatenate([blocks[1:], head_block[None]], 0)
    result = jnp.einsum("ji,bjr->bir", lower_block, blocks, precision=lax.Precision.HIGHEST)
    result = result + jnp.einsum(
        "ji,bjr->bir", upper_block, following, precision=lax.Precision.HIGHEST
    )
    return result.reshape(values.shape)


def shards(design, observed, slab_counts, gap_mask, filter_taps, kaula_diag, precond):
    epoch_rows, coef_rows = design.shape
    owned_rows = coef_rows // lax.axis_size("tm")
    owner_index = lax.axis_index("tm")
    lower_block, upper_block = block_pair(filter_taps)
    position = jnp.arange(epoch_rows, dtype=jnp.int32)
    weight = ((gap_mask == 1) & (position < slab_counts[0])).astype(jnp.float32)[:, None]

    def weighted(values):
        inner = forward(weight * values, lower_block, upper_block)
        return (weight * backward(inner, lower_block, upper_block)).astype(jnp.bfloat16)

    def transposed_term(filtered):
        return lax.dot_general(
            design, filtered, (((0,), (0,)), ((), ())), preferred_element_type=jnp.float32
        )

    def collect_rows(filtered):
        return lax.psum_scatter(transposed_term(filtered), "tm", scatter_dimension=0, tiled=True)

    def global_sum(terms):
        return lax.psum(terms, ("tm", "coef"))

    kaula_col = lax.dynamic_slice_in_dim(kaula_diag, owner_index * owned_rows, owned_rows, 0)[
        :, None
    ]
    precond_col = lax.dynamic_slice_in_dim(precond, owner_index * owned_rows, owned_rows, 0)[
        :, None
    ]
    residual = collect_rows(weighted(observed))
    solution = jnp.zeros_like(residual)
    scaled = precond_col * residual
    direction = scaled
    norm_now = global_sum(jnp.sum(residual * scaled, 0))
    for iteration in range(ITERS):
        slab_values = lax.psum(
            jnp.dot(
                design,
                lax.all_gather(direction.astype(jnp.bfloat16), "tm", axis=0, tiled=True),
                preferred_element_type=jnp.float32,
            ),
            "coef",
        )
        image = collect_rows(weighted(slab_values)) + kaula_col * direction
        curvature = global_sum(jnp.sum(direction * image, 0))
        step_len = norm_now / curvature
        solution = solution + step_len * direction
        residual = residual - step_len * image
        if iteration + 1 < ITERS:
            scaled = precond_col * residual
            norm_next = global_sum(jnp.sum(residual * scaled, 0))
            direction = scaled + norm_next / norm_now * direction
            norm_now = norm_next
    return (solution, residual)


def solution(mesh):
    placed = (P("tm", "coef"), P("tm", None), P("tm"), P("tm"), P(), P("coef"), P("coef"))
    return jax.shard_map(
        shards,
        mesh=mesh,
        in_specs=placed,
        out_specs=(P(("coef", "tm"), None), P(("coef", "tm"), None)),
        check_vma=False,
    )
```

profile of v0, /device:TPU:0, one launch (start us, length us, event | category | flops | bytes accessed | tf_op | source)
XLA Modules:
  0.0 791.0 jit_solution(16113411345253262551)
XLA Ops:
  9.6 4.9 collective-permute-start
  17.5 1.3 collective-permute-start.1
  19.1 4.5 collective-permute-done.1
  24.1 6.5 convolution_bitcast_fusion.2
  30.6 8.0 %copy.74 = f32[12544,128]{1,0:T(8,128)} copy(f32[12544,128]{0,1:T(8,128)} %convolution_bitcast_fusion.2) | data formatting | bytes 12845056
  39.4 120.5 %reduce-scatter.10.cloned.1.call-done = f32[1568,128]{1,0:T(8,128)} async-done(((f32[12544,128]{1,0:T(8,128)}), f32[1568,128]{1,0:T(8,128)}) %reduce-scatter.10.cloned.1.call-update) | async-done | bytes 802832
  159.9 1.4 copy.75
  162.4 60.2 %all-gather.3.cloned.1.call-done = bf16[12544,128]{1,0:T(8,128)(2,1)} async-done(((bf16[1568,128]{1,0:T(8,128)(2,1)}), bf16[12544,128]{1,0:T(8,128)(2,1)}) %all-gather.3.cloned.1.call-update) | async-done | bytes 3211280 | tf_op jit(solution)/shard_map/all_gather | solution.py:91
  222.6 6.7 convolution_bitcast_fusion.4
  229.3 30.5 %all-reduce.4.cloned.1.call-done = f32[256,128]{0,1:T(8,128)} async-done(((f32[256,128]{0,1:T(8,128)}), f32[256,128]{0,1:T(8,128)}) %all-reduce.4.cloned.1.call-update) | async-done | bytes 131088 | tf_op jit(solution)/shard_map/psum | solution.py:88
  260.8 3.4 collective-permute-start.2
  266.4 1.3 collective-permute-start.3
  268.0 4.9 collective-permute-done.3
  273.3 6.5 convolution_bitcast_fusion.1
  279.8 8.0 %copy.76 = f32[12544,128]{1,0:T(8,128)} copy(f32[12544,128]{0,1:T(8,128)} %convolution_bitcast_fusion.1) | data formatting | bytes 12845056
  288.7 119.7 %reduce-scatter.12.cloned.1.call-done = f32[1568,128]{1,0:T(8,128)} async-done(((f32[12544,128]{1,0:T(8,128)}), f32[1568,128]{1,0:T(8,128)}) %reduce-scatter.12.cloned.1.call-update) | async-done | bytes 802832
  408.4 1.4 copy.77
  410.2 39.5 %all-reduce = (f32[128]{0:T(128)S(1)}, f32[128]{0:T(128)S(1)}) all-reduce(f32[128]{0:T(128)S(1)} %get-tuple-element.7, f32[128]{0:T(128)S(1)} %get-tuple-element.6), channel_id=1, replica_groups=mesh['tm'=8,'coef'=4] {'tm','coef'}, use_global_device_ids=true, to_apply=%region_2.0 | all-reduce | flops 256 | bytes 2048 | tf_op jit(solution)/shard_map/psum | solution.py:74
  450.0 39.6 %psum.45 = f32[128]{0:T(128)S(1)} all-reduce(f32[128]{0:T(128)S(1)} %fusion.7), channel_id=1, replica_groups=mesh['tm'=8,'coef'=4] {'tm','coef'}, use_global_device_ids=true, to_apply=%region_8.0 | all-reduce | flops 128 | bytes 1024 | tf_op jit(solution)/shard_map/psum | solution.py:74
  491.2 60.7 %all-gather.5.cloned.1.call-done = bf16[12544,128]{1,0:T(8,128)(2,1)} async-done(((bf16[1568,128]{1,0:T(8,128)(2,1)}), bf16[12544,128]{1,0:T(8,128)(2,1)}) %all-gather.5.cloned.1.call-update) | async-done | bytes 3211280 | tf_op jit(solution)/shard_map/all_gather | solution.py:91
  551.9 6.7 convolution_bitcast_fusion.3
  558.6 30.6 %all-reduce.6.cloned.1.call-done = f32[256,128]{0,1:T(8,128)} async-done(((f32[256,128]{0,1:T(8,128)}), f32[256,128]{0,1:T(8,128)}) %all-reduce.6.cloned.1.call-update) | async-done | bytes 131088 | tf_op jit(solution)/shard_map/psum | solution.py:88
  590.1 3.4 collective-permute-start.4
  595.7 1.3 collective-permute-start.5
  597.3 4.9 collective-permute-done.5
  602.6 6.5 convolution_bitcast_fusion
  609.2 8.0 %copy.78 = f32[12544,128]{1,0:T(8,128)} copy(f32[12544,128]{0,1:T(8,128)} %convolution_bitcast_fusion) | data formatting | bytes 12845056
  617.2 120.6 %reduce-scatter.14.cloned.1.call-done = f32[1568,128]{1,0:T(8,128)} async-done(((f32[12544,128]{1,0:T(8,128)}), f32[1568,128]{1,0:T(8,128)}) %reduce-scatter.14.cloned.1.call-update) | async-done | bytes 802832
  737.8 1.4 copy.79
  739.7 39.5 %psum.47 = f32[128]{0:T(128)S(1)} all-reduce(f32[128]{0:T(128)S(1)} %multiply_reduce_fusion), channel_id=1, replica_groups=mesh['tm'=8,'coef'=4] {'tm','coef'}, use_global_device_ids=true, to_apply=%region_12.0 | all-reduce | flops 128 | bytes 1024 | tf_op jit(solution)/shard_map/psum | solution.py:74
  779.2 1.5 multiply_subtract_fusion
  780.7 2.3 copy.52
  (65 shorter events, 19.7 us)
Async XLA Ops:
  7.2 152.8 %reduce-scatter.10.cloned.1.call-start = ((), (), s32[]{:S(2)}) async-start(), calls=%async_computation.7 | async-start | bytes 7225344
  9.6 7.6 collective-permute-start
  17.5 6.2 collective-permute-start.1
  38.6 184.0 %all-gather.3.cloned.1.call-start = ((), (), s32[]{:S(2)}) async-start(), calls=%async_computation.3 | async-start | bytes 3612672 | tf_op jit(solution)/shard_map/all_gather | solution.py:91
  162.4 97.5 %all-reduce.4.cloned.1.call-start = ((), (), s32[]{:S(2)}) async-start(), calls=%async_computation.4 | async-start | bytes 262144 | tf_op jit(solution)/shard_map/psum | solution.py:88
  229.3 179.1 %reduce-scatter.12.cloned.1.call-start = ((), (), s32[]{:S(2)}) async-start(), calls=%async_computation.8 | async-start | bytes 7225344
  260.8 5.3 collective-permute-start.2
  266.4 6.5 collective-permute-start.3
  287.8 264.0 %all-gather.5.cloned.1.call-start = ((), (), s32[]{:S(2)}) async-start(), calls=%async_computation.5 | async-start | bytes 3612672 | tf_op jit(solution)/shard_map/all_gather | solution.py:91
  490.9 98.3 %all-reduce.6.cloned.1.call-start = ((), (), s32[]{:S(2)}) async-start(), calls=%async_computation.6 | async-start | bytes 262144 | tf_op jit(solution)/shard_map/psum | solution.py:88
  558.6 179.2 %reduce-scatter.14.cloned.1.call-start = ((), (), s32[]{:S(2)}) async-start(), calls=%async_computation.9 | async-start | bytes 7225344
  590.1 5.3 collective-permute-start.4
  595.7 6.5 collective-permute-start.5
Sparse Core Ops, SparseCore 0:
  38.7 121.1 reduce-scatter.9
  162.7 59.8 all-gather.2
  229.4 30.4 all-reduce.3
  288.0 120.4 reduce-scatter.11
  491.1 60.7 all-gather.4
  558.7 30.4 all-reduce.5
  617.3 120.4 reduce-scatter.13
where the time goes:
time: 792 us; the launch traced here: 791 us
  waiting for transfers between devices  559 us (71%)
  blocking collectives  119 us (15%)
  matrix products  38.3 us (5%)
  local copies, waits for them, and re-layouts  38.1 us (5%)
  starting transfers between devices  16 us (2%)
  between operations  15.1 us (2%)
    unnamed x10, waiting for transfers between devices  361 us
    all_gather x2, waiting for transfers between devices, shards(): lax.all_gather(direction.astype(jnp.bfloat16), 'tm', axis=0, tiled=True)  121 us
    psum x3, blocking collectives, global_sum(): return lax.psum(terms, ('tm', 'coef'))  119 us
    psum x2, waiting for transfers between devices, shards(): lax.psum(jnp.dot(design, lax.all_gather(direction.astype(jnp.bfloat16), '...  61.1 us
    unnamed x12, local copies, waits for them, and re-layouts  32.9 us
    dot_general x3, matrix products, transposed_term(): lax.dot_general(design, filtered, (((0,), (0,)), ((), ())), preferred_ele...  19.6 us
  transfers between devices with their start and end apart: 13, of which 12 were waited for; matrix products, arithmetic and copies ran while one was open for 1% of the time, Pallas kernels for 0%

commit v1 on v0

--- a/solution.py
+++ b/solution.py
@@ -85,7 +85,12 @@
     direction = scaled
     norm_now = global_sum(jnp.sum(residual * scaled, 0))
     for iteration in range(ITERS):
-        slab_values = lax.psum(
+
+        def draw_chunk_for(local, link_axis):
+            newest = lax.all_gather(local, link_axis).sum(axis=0)
+            return newest
+
+        slab_values = draw_chunk_for(
             jnp.dot(
                 design,
                 lax.all_gather(direction.astype(jnp.bfloat16), "tm", axis=0, tiled=True),

time: 792 us -> 742 us (0.937)
  waiting for transfers between devices: 559 us -> 500 us
  blocking collectives: 119 us -> 133 us
    psum x2 -> x0, waiting for transfers between devices: 61.1 us -> none  [shards(): lax.psum(jnp.dot(design, lax.all_gather(direction.astype(jnp.bfloat16), '...]
    all_gather x0 -> x2, blocking collectives: none -> 14.3 us  [draw_chunk_for(): newest = lax.all_gather(local, link_axis).sum(axis=0)]
    unnamed x10 -> x8, waiting for transfers between devices: 361 us -> 362 us
    unnamed x12 -> x14, local copies, waits for them, and re-layouts: 32.9 us -> 32.9 us
  transfers between devices with their start and end apart: 13 -> 11, of which waited for: 12 -> 10; matrix products, arithmetic and copies ran while one was open for 1% -> 1% of each run, Pallas kernels for 0% -> 0%
where the time goes in v1:
time: 742 us; the launch traced here: 741 us
  waiting for transfers between devices  500 us (67%)
  blocking collectives  133 us (18%)
  local copies, waits for them, and re-layouts  38.6 us (5%)
  matrix products  35.2 us (5%)
  between operations  14.8 us (2%)
  starting transfers between devices  14.1 us (2%)
    unnamed x8, waiting for transfers between devices  362 us
    all_gather x2, waiting for transfers between devices, shards(): lax.all_gather(direction.astype(jnp.bfloat16), 'tm', axis=0, tiled=True)  121 us
    psum x3, blocking collectives, global_sum(): return lax.psum(terms, ('tm', 'coef'))  119 us
    unnamed x14, local copies, waits for them, and re-layouts  32.9 us
    dot_general x3, matrix products, transposed_term(): lax.dot_general(design, filtered, (((0,), (0,)), ((), ())), preferred_ele...  19.6 us
    ppermute x6, waiting for transfers between devices, shifted(): lax.ppermute(value, axis, [(source, source + steps) for source in range(f...  17.7 us
  transfers between devices with their start and end apart: 11, of which 10 were waited for; matrix products, arithmetic and copies ran while one was open for 1% of the time, Pallas kernels for 0%

profile of v1, /device:TPU:0, one launch (start us, length us, event | category | flops | bytes accessed | tf_op | source)
XLA Modules:
  0.0 741.0 jit_solution(13712562836502647577)
XLA Ops:
  9.6 4.9 collective-permute-start
  17.5 1.3 collective-permute-start.1
  19.1 4.5 collective-permute-done.1
  24.1 6.5 convolution_bitcast_fusion.2
  30.6 8.0 %copy.74 = f32[12544,128]{1,0:T(8,128)} copy(f32[12544,128]{0,1:T(8,128)} %convolution_bitcast_fusion.2) | data formatting | bytes 12845056
  39.5 120.8 %reduce-scatter.10.cloned.1.call-done = f32[1568,128]{1,0:T(8,128)} async-done(((f32[12544,128]{1,0:T(8,128)}), f32[1568,128]{1,0:T(8,128)}) %reduce-scatter.10.cloned.1.call-update) | async-done | bytes 802832
  160.3 1.4 copy.75
  162.8 60.1 %all-gather.5.cloned.1.call-done = bf16[12544,128]{1,0:T(8,128)(2,1)} async-done(((bf16[1568,128]{1,0:T(8,128)(2,1)}), bf16[12544,128]{1,0:T(8,128)(2,1)}) %all-gather.5.cloned.1.call-update) | async-done | bytes 3211280 | tf_op jit(solution)/shard_map/all_gather | solution.py:96
  223.0 6.0 convolution_bitcast_fusion.4
  229.0 7.1 all-gather
  236.8 2.5 collective-permute-start.2
  239.5 1.6 collective-permute-done.2
  243.0 5.0 collective-permute-done.3
  248.4 6.5 convolution_bitcast_fusion.1
  255.0 8.0 %copy.76 = f32[12544,128]{1,0:T(8,128)} copy(f32[12544,128]{0,1:T(8,128)} %convolution_bitcast_fusion.1) | data formatting | bytes 12845056
  263.8 120.0 %reduce-scatter.12.cloned.1.call-done = f32[1568,128]{1,0:T(8,128)} async-done(((f32[12544,128]{1,0:T(8,128)}), f32[1568,128]{1,0:T(8,128)}) %reduce-scatter.12.cloned.1.call-update) | async-done | bytes 802832
  383.8 1.4 copy.77
  385.6 39.5 %all-reduce = (f32[128]{0:T(128)S(1)}, f32[128]{0:T(128)S(1)}) all-reduce(f32[128]{0:T(128)S(1)} %get-tuple-element.7, f32[128]{0:T(128)S(1)} %get-tuple-element.6), channel_id=1, replica_groups=mesh['tm'=8,'coef'=4] {'tm','coef'}, use_global_device_ids=true, to_apply=%region_2.0 | all-reduce | flops 256 | bytes 2048 | tf_op jit(solution)/shard_map/psum | solution.py:74
  425.4 39.6 %psum.30 = f32[128]{0:T(128)S(1)} all-reduce(f32[128]{0:T(128)S(1)} %fusion.7), channel_id=1, replica_groups=mesh['tm'=8,'coef'=4] {'tm','coef'}, use_global_device_ids=true, to_apply=%region_8.0 | all-reduce | flops 128 | bytes 1024 | tf_op jit(solution)/shard_map/psum | solution.py:74
  466.6 60.7 %all-gather.7.cloned.1.call-done = bf16[12544,128]{1,0:T(8,128)(2,1)} async-done(((bf16[1568,128]{1,0:T(8,128)(2,1)}), bf16[12544,128]{1,0:T(8,128)(2,1)}) %all-gather.7.cloned.1.call-update) | async-done | bytes 3211280 | tf_op jit(solution)/shard_map/all_gather | solution.py:96
  527.3 6.0 convolution_bitcast_fusion.3
  533.3 7.1 all-gather.1
  541.0 2.5 collective-permute-start.4
  543.8 1.6 collective-permute-done.4
  547.3 5.0 collective-permute-done.5
  552.7 6.5 convolution_bitcast_fusion
  559.2 8.0 %copy.78 = f32[12544,128]{1,0:T(8,128)} copy(f32[12544,128]{0,1:T(8,128)} %convolution_bitcast_fusion) | data formatting | bytes 12845056
  567.2 120.9 %reduce-scatter.14.cloned.1.call-done = f32[1568,128]{1,0:T(8,128)} async-done(((f32[12544,128]{1,0:T(8,128)}), f32[1568,128]{1,0:T(8,128)}) %reduce-scatter.14.cloned.1.call-update) | async-done | bytes 802832
  688.1 1.4 copy.79
  690.0 39.5 %psum.31 = f32[128]{0:T(128)S(1)} all-reduce(f32[128]{0:T(128)S(1)} %multiply_reduce_fusion), channel_id=1, replica_groups=mesh['tm'=8,'coef'=4] {'tm','coef'}, use_global_device_ids=true, to_apply=%region_12.0 | all-reduce | flops 128 | bytes 1024 | tf_op jit(solution)/shard_map/psum | solution.py:74
  729.5 1.5 multiply_subtract_fusion
  731.0 2.3 copy.52
  (68 shorter events, 18.3 us)
Async XLA Ops:
  7.2 153.1 %reduce-scatter.10.cloned.1.call-start = ((), (), s32[]{:S(2)}) async-start(), calls=%async_computation.5 | async-start | bytes 7225344
  9.6 7.6 %collective-permute-start = (f32[128,128]{0,1:T(8,128)S(1)}, f32[128,128]{0,1:T(8,128)S(1)}, u32[]{:S(2)}, u32[]{:S(2)}) collective-permute-start(f32[128,128]{0,1:T(8,128)S(1)} %get-tuple-element.22), channel_id=1, source_target_pairs={{0,4},{4,8},{8,12},{12,16},{16,20},{20,24},{24,28},{1,5},{5,9},{9,... | collective-permute-start | bytes 196616 | tf_op jit(solution)/shard_map/ppermute | solution.py:12
  17.5 6.2 collective-permute-start.1
  38.6 124.2 %copy-start = (s32[256]{0:T(256)S(1)}, s32[256]{0:T(256)}, u32[]{:S(2)}) copy-start(s32[256]{0:T(256)} %param.10) | copy-start | bytes 3076
  38.6 184.4 %all-gather.5.cloned.1.call-start = ((), (), s32[]{:S(2)}) async-start(), calls=%async_computation.3 | async-start | bytes 3612672 | tf_op jit(solution)/shard_map/all_gather | solution.py:96
  162.8 221.1 %reduce-scatter.12.cloned.1.call-start = ((), (), s32[]{:S(2)}) async-start(), calls=%async_computation.6 | async-start | bytes 7225344
  236.8 4.3 collective-permute-start.2
  241.4 6.6 collective-permute-start.3
  263.0 264.3 %all-gather.7.cloned.1.call-start = ((), (), s32[]{:S(2)}) async-start(), calls=%async_computation.4 | async-start | bytes 3612672 | tf_op jit(solution)/shard_map/all_gather | solution.py:96
  466.3 221.8 %reduce-scatter.14.cloned.1.call-start = ((), (), s32[]{:S(2)}) async-start(), calls=%async_computation.7 | async-start | bytes 7225344
  541.0 4.3 collective-permute-start.4
  545.7 6.6 collective-permute-start.5
Sparse Core Ops, SparseCore 0:
  38.7 121.5 reduce-scatter.9
  163.1 59.8 all-gather.4
  263.1 120.7 reduce-scatter.11
  466.5 60.7 all-gather.6
  567.4 120.7 reduce-scatter.13
